TPU v7x, 32 devices: a whole 2x2x4 slice. The times are simulated.
32 devices in a mesh: front: 2 (over core), row: 4 (over y, x), col: 4 (over z).
Axes of the slice: x: 2, y: 2, z: 4, core: 2. Of those that a mesh axis runs over, the one named last changes fastest.
Arguments:
- front_rows: float32 [4096, 24576], P(('front', 'row'), 'col'), parts along dimension 0, may hold values from -0.0546875 to 0.0546875
- random_columns: bfloat16 [49152, 512], P(('front', 'col'), 'row'), parts along dimension 0, may hold values from -6 to 6
Outputs:
- basis: float32 [4096, 256], P(('front', 'row', 'col')), parts along dimension 0
- projected: float32 [1024, 512], P(('front', 'row')), parts along dimension 0
There are 2 independent parts, one for each index of `front`. A program takes and returns all parts, laid end to end along the dimension named above; each array names one. Nothing has to cross between parts.
All inputs are finite; a program needn't handle non-finite values.
Results may differ from a plain program's by a relative error of at most 0.0003.
Values may be sent and summed in bfloat16 or wider, within the bound.
A program may use at most 64 MiB of HBM per device.

v0:
```python
import jax
import jax.numpy as jnp
from jax import lax
from jax.sharding import PartitionSpec as P

RANK = 256


def partner(value, axis, stride):
    mask = 2**stride
    pairs = [(source, source ^ mask) for source in range(lax.axis_size(axis))]
    return lax.ppermute(value, axis, pairs)


def inner_rows(left, right):
    return lax.dot_general(
        left,
        right,
        (((0,), (0,)), ((), ())),
        precision=lax.Precision.HIGHEST,
        preferred_element_type=jnp.float32,
    )


def leaf_total(partial_gram):
    return partial_gram + partner(partial_gram, "row", 0)


def per_device(front_rows, random_columns):
    block_rows = front_rows.shape[0]
    col_count = lax.axis_size("col")
    col_index = lax.axis_index("col")
    row_index = lax.axis_index("row")
    own_rows = block_rows // col_count
    partial_value = jnp.dot(
        front_rows,
        lax.all_gather(random_columns, "row", axis=1, tiled=True).astype(jnp.float32),
        precision=lax.Precision.HIGHEST,
        preferred_element_type=jnp.float32,
    )
    whole = lax.psum(partial_value, "col")
    local_gram = inner_rows(whole[:, :RANK], whole)
    mine = lax.dynamic_slice_in_dim(whole, col_index * own_rows, own_rows, 0)
    gram = leaf_total(local_gram)
    lower = jnp.linalg.cholesky(gram[:, :RANK])
    basis = lax.linalg.triangular_solve(
        lower, mine[:, :RANK], left_side=False, lower=True, transpose_a=True
    )
    coupling = lax.linalg.triangular_solve(lower, gram, left_side=True, lower=True)
    half = RANK // 2
    projected = lax.dynamic_slice_in_dim(coupling, row_index % 2 * half, half, 0)
    return (basis, projected)


def solution(mesh):
    return jax.shard_map(
        per_device,
        mesh=mesh,
        in_specs=(P(("front", "row"), "col"), P(("front", "col"), "row")),
        out_specs=(P(("front", "row", "col"), None), P(("front", "row"), None)),
        check_vma=False,
    )
```

profile of v0, /device:TPU:0, one launch (start us, length us, event | category | flops | bytes accessed | tf_op | source)
XLA Modules:
  0.0 239.0 jit_solution(649683142217514492)
XLA Ops:
  7.2 0.0 all-gather.2.cloned.1.call-start
  7.2 0.7 all-gather.2.cloned.1.call-update
  7.9 0.0 all-reduce.3.cloned.1.call-start
  7.9 74.5 %all-gather.2.cloned.1.call-done = bf16[6144,512]{1,0:T(8,128)(2,1)} async-done(((bf16[6144,128]{1,0:T(8,128)(2,1)}), bf16[6144,512]{1,0:T(8,128)(2,1)}) %all-gather.2.cloned.1.call-update) | async-done | bytes 6291472 | tf_op jit(solution)/shard_map/all_gather | solution.py:37
  82.4 14.8 %fusion.18 = f32[512,512]{1,0:T(8,128)} fusion(f32[512,6144]{1,0:T(8,128)} %param.2, bf16[6144,512]{1,0:T(8,128)(2,1)} %all-gather.2.cloned.1.call-done), kind=kOutput, calls=%fused_computation.41 | convolution fusion | flops 19327352832 | bytes 19922944 | tf_op jit(solution)/shard_map/dot_general | solution.py:35
  97.2 0.0 all-reduce.3.cloned.1.call-update
  97.3 52.1 %all-reduce.3.cloned.1.call-done = f32[512,512]{1,0:T(8,128)} async-done(((f32[512,512]{1,0:T(8,128)}), f32[512,512]{1,0:T(8,128)}) %all-reduce.3.cloned.1.call-update) | async-done | bytes 1048592 | tf_op jit(solution)/shard_map/psum | solution.py:41
  149.3 3.2 %fusion = f32[256,512]{0,1:T(8,128)S(1)} fusion(f32[512,512]{1,0:T(8,128)} %all-reduce.3.cloned.1.call-done), kind=kOutput, calls=%fused_computation.4 | convolution fusion | flops 805306368 | bytes 2097152 | tf_op jit(solution)/shard_map/dot_general | solution.py:16
  152.5 1.5 collective-permute-start
  154.1 12.3 %collective-permute-done = f32[256,512]{0,1:T(8,128)S(1)} collective-permute-done((f32[256,512]{0,1:T(8,128)S(1)}, f32[256,512]{0,1:T(8,128)S(1)}, u32[]{:S(2)}, u32[]{:S(2)}) %collective-permute-start) | collective-permute-done | bytes 524320 | tf_op jit(solution)/shard_map/ppermute | solution.py:12
  166.4 0.1 add.40
  166.5 0.1 copy.6
  166.7 11.7 %cholesky.50 = f32[128,128]{1,0:T(8,128)S(1)} custom-call(f32[128,128]{1,0:T(8,128)S(1)} %cholesky.118), custom_call_target="Cholesky" | custom-call | tf_op jit(solution)/shard_map/jit(cholesky)/cholesky | solution.py:45
  178.4 9.8 %custom-call.16 = f32[1,128,128]{1,2,0:T(8,128)S(1)} custom-call(f32[1,128,128]{2,1,0:T(8,128)S(1)} %get-tuple-element.25), custom_call_target="InvertDiagBlocksLowerTriangular" | custom-call | tf_op jit(solution)/shard_map/jit(cholesky)/cholesky | solution.py:45
  188.3 0.2 constant_dynamic-update-slice_fusion
  188.5 0.3 convolution_subtract_fusion.1
  188.7 11.9 %cholesky.105 = f32[128,128]{1,0:T(8,128)S(1)} custom-call(f32[128,128]{1,0:T(8,128)S(1)} %convolution_subtract_fusion.1), custom_call_target="Cholesky" | custom-call | tf_op jit(solution)/shard_map/jit(cholesky)/cholesky | solution.py:45
  200.6 0.7 compare_reduce_fusion
  202.7 0.1 triangular_solve.73
  202.8 4.1 %while.1 = (s32[]{:T(128)}, f32[256,256]{1,0:T(8,128)S(1)}, s32[2,2]{1,0:T(2,128)S(1)}, f32[2,128,128]{2,1,0:T(8,128)S(1)}, s32[]{:T(128)}) while((s32[]{:T(128)}, f32[256,256]{1,0:T(8,128)S(1)}, s32[2,2]{1,0:T(2,128)S(1)}, f32[2,128,128]{2,1,0:T(8,128)S(1)}, s32[]{:T(128)}) %tuple.28), condition=%wide.while_cond, body=%wide.while_body.sunk | while | flops 2 | bytes 131181 | solution.py:46
  202.8 0.6 fusion.28
  203.4 1.4 bitcast_dynamic-update-slice_fusion.2
  204.9 0.6 fusion.28
  205.5 1.4 bitcast_dynamic-update-slice_fusion.2
  206.9 19.7 %custom-call.17 = f32[2,128,128]{1,2,0:T(8,128)S(1)} custom-call(f32[2,128,128]{2,1,0:T(8,128)S(1)} %get-tuple-element.9), custom_call_target="InvertDiagBlocksLowerTriangular" | custom-call | tf_op jit(solution)/shard_map/triangular_solve | solution.py:46
  226.6 0.4 fusion.4
  227.0 0.6 fusion.13
  227.6 0.4 fusion.3
  228.0 1.1 fusion.9
  229.2 1.1 convolution_subtract_fusion
  230.3 0.3 fusion.12
  230.6 0.8 copy.7
  231.4 0.8 fusion.2
  (12 shorter events, 0.2 us)
Async XLA Ops:
  7.2 75.3 %all-gather.2.cloned.1.call-start = ((), (), s32[]{:S(2)}) async-start(), calls=%async_computation | async-start | bytes 7864320 | tf_op jit(solution)/shard_map/all_gather | solution.py:37
  7.9 141.4 %all-reduce.3.cloned.1.call-start = ((), (), s32[]{:S(2)}) async-start(), calls=%async_computation.1 | async-start | bytes 2097152 | tf_op jit(solution)/shard_map/psum | solution.py:41
  152.5 13.8 %collective-permute-start = (f32[256,512]{0,1:T(8,128)S(1)}, f32[256,512]{0,1:T(8,128)S(1)}, u32[]{:S(2)}, u32[]{:S(2)}) collective-permute-start(f32[256,512]{0,1:T(8,128)S(1)} %fusion), channel_id=1, source_target_pairs={{0,4},{4,0},{8,12},{12,8},{1,5},{5,1},{9,13},{13,9},{2,6},{6,2},{1... | collective-permute-start | bytes 1572872 | tf_op jit(solution)/shard_map/ppermute | solution.py:12
Sparse Core Ops, SparseCore 0:
  9.8 72.6 all-gather.1
  97.4 51.8 all-reduce.2
where the time goes:
time: 239 us
  waiting for transfers between devices  140 us (59%)
  other arithmetic  54.7 us (23%)
  matrix products  22.5 us (9%)
  between operations  15.5 us (6%)
  local copies, waits for them, and re-layouts  5.06 us (2%)
    all_gather x1, waiting for transfers between devices, per_device(): lax.all_gather(random_columns, 'row', axis=1, tiled=True)  74.5 us
    psum x1, waiting for transfers between devices, per_device(): whole = lax.psum(partial_value, 'col')  52.1 us
    another operation x6, other arithmetic, per_device(): lower = jnp.linalg.cholesky(gram[:, :RANK])  34.2 us
    another operation x4, other arithmetic, per_device(): lax.linalg.triangular_solve(lower, mine[:, :RANK], left_side=False, lower...  19.7 us
    dot_general x1, matrix products, per_device(): jnp.dot(front_rows, lax.all_gather(random_columns, 'row', axis=1, tiled=T...  14.8 us
    ppermute x1, waiting for transfers between devices, partner(): return lax.ppermute(value, axis, pairs)  12.3 us
  transfers between devices with their start and end apart: 3, of which 3 were waited for; matrix products, arithmetic and copies ran while one was open for 0% of the time, Pallas kernels for 0%

commit v1 on v0

--- a/solution.py
+++ b/solution.py
@@ -38,7 +38,12 @@
         precision=lax.Precision.HIGHEST,
         preferred_element_type=jnp.float32,
     )
-    whole = lax.psum(partial_value, "col")
+    whole, all_values = (partial_value, 0)
+    nd = lax.axis_size("col")
+    while 1 << all_values < nd:
+        r1 = lax.ppermute(whole, "col", [(src_i, src_i ^ 1 << all_values) for src_i in range(nd)])
+        whole = whole + r1
+        all_values = all_values + 1
     local_gram = inner_rows(whole[:, :RANK], whole)
     mine = lax.dynamic_slice_in_dim(whole, col_index * own_rows, own_rows, 0)
     gram = leaf_total(local_gram)

time: 239 us -> 254 us (1.063)
  waiting for transfers between devices: 140 us -> 155 us
  starting transfers between devices: 1.61 us -> 5.58 us
  matrix products: 22.5 us -> 18.6 us
    ppermute x0 -> x2, waiting for transfers between devices: none -> 68.1 us  [per_device(): lax.ppermute(whole, 'col', [(src_i, src_i ^ 1 << all_values) for src_i in...]
    psum x1 -> x0, waiting for transfers between devices: 52.1 us -> none  [per_device(): whole = lax.psum(partial_value, 'col')]
    ppermute x0 -> x2, starting transfers between devices: none -> 4.02 us  [per_device(): lax.ppermute(whole, 'col', [(src_i, src_i ^ 1 << all_values) for src_i in...]
  transfers between devices with their start and end apart: 3 -> 4, of which waited for: 3 -> 4; matrix products, arithmetic and copies ran while one was open for 0% -> 0% of each run, Pallas kernels for 0% -> 0%
where the time goes in v1:
time: 254 us
  waiting for transfers between devices  155 us (61%)
  other arithmetic  55.1 us (22%)
  matrix products  18.6 us (7%)
  between operations  15.4 us (6%)
  starting transfers between devices  5.58 us (2%)
  local copies, waits for them, and re-layouts  4.78 us (2%)
    all_gather x1, waiting for transfers between devices, per_device(): lax.all_gather(random_columns, 'row', axis=1, tiled=True)  74.6 us
    ppermute x2, waiting for transfers between devices, per_device(): lax.ppermute(whole, 'col', [(src_i, src_i ^ 1 << all_values) for src_i in...  68.1 us
    another operation x6, other arithmetic, per_device(): lower = jnp.linalg.cholesky(gram[:, :RANK])  34.1 us
    another operation x4, other arithmetic, per_device(): lax.linalg.triangular_solve(lower, mine[:, :RANK], left_side=False, lower...  19.7 us
    dot_general x1, matrix products, per_device(): jnp.dot(front_rows, lax.all_gather(random_columns, 'row', axis=1, tiled=T...  14 us
    ppermute x1, waiting for transfers between devices, partner(): return lax.ppermute(value, axis, pairs)  11.5 us
  transfers between devices with their start and end apart: 4, of which 4 were waited for; matrix products, arithmetic and copies ran while one was open for 0% of the time, Pallas kernels for 0%

profile of v1, /device:TPU:0, one launch (start us, length us, event | category | flops | bytes accessed | tf_op | source)
XLA Modules:
  0.0 254.3 jit_solution(11963640298133697085)
XLA Ops:
  7.2 0.0 all-gather.2.cloned.1.call-start
  7.2 0.7 all-gather.2.cloned.1.call-update
  7.9 74.6 %all-gather.2.cloned.1.call-done = bf16[6144,512]{1,0:T(8,128)(2,1)} async-done(((bf16[6144,128]{1,0:T(8,128)(2,1)}), bf16[6144,512]{1,0:T(8,128)(2,1)}) %all-gather.2.cloned.1.call-update) | async-done | bytes 6291472 | tf_op jit(solution)/shard_map/all_gather | solution.py:37
  82.4 14.0 %fusion.19 = f32[512,512]{1,0:T(8,128)S(1)} fusion(f32[512,6144]{1,0:T(8,128)} %param.2, bf16[6144,512]{1,0:T(8,128)(2,1)} %all-gather.2.cloned.1.call-done), kind=kOutput, calls=%fused_computation.42 | convolution fusion | flops 19327352832 | bytes 19922944 | tf_op jit(solution)/shard_map/dot_general | solution.py:35
  96.4 1.6 collective-permute-start
  98.0 23.2 %collective-permute-done = f32[512,512]{1,0:T(8,128)S(1)} collective-permute-done((f32[512,512]{1,0:T(8,128)S(1)}, f32[512,512]{1,0:T(8,128)S(1)}, u32[]{:S(2)}, u32[]{:S(2)}) %collective-permute-start) | collective-permute-done | bytes 1048608 | tf_op jit(solution)/shard_map/ppermute | solution.py:44
  121.2 0.2 add.43
  121.5 2.5 collective-permute-start.1
  123.9 44.8 %collective-permute-done.1 = f32[512,512]{1,0:T(8,128)S(1)} collective-permute-done((f32[512,512]{1,0:T(8,128)S(1)}, f32[512,512]{1,0:T(8,128)S(1)}, u32[]{:S(2)}, u32[]{:S(2)}) %collective-permute-start.1) | collective-permute-done | bytes 1048608 | tf_op jit(solution)/shard_map/ppermute | solution.py:44
  168.8 0.2 add.44
  169.0 1.8 fusion
  170.8 1.5 collective-permute-start.2
  172.3 11.5 %collective-permute-done.2 = f32[256,512]{0,1:T(8,128)S(1)} collective-permute-done((f32[256,512]{0,1:T(8,128)S(1)}, f32[256,512]{0,1:T(8,128)S(1)}, u32[]{:S(2)}, u32[]{:S(2)}) %collective-permute-start.2) | collective-permute-done | bytes 524320 | tf_op jit(solution)/shard_map/ppermute | solution.py:12
  183.8 0.1 add.46
  183.9 0.1 copy.6
  184.1 11.7 %cholesky.50 = f32[128,128]{1,0:T(8,128)S(1)} custom-call(f32[128,128]{1,0:T(8,128)S(1)} %cholesky.118), custom_call_target="Cholesky" | custom-call | tf_op jit(solution)/shard_map/jit(cholesky)/cholesky | solution.py:50
  195.8 9.8 %custom-call.16 = f32[1,128,128]{1,2,0:T(8,128)S(1)} custom-call(f32[1,128,128]{2,1,0:T(8,128)S(1)} %get-tuple-element.25), custom_call_target="InvertDiagBlocksLowerTriangular" | custom-call | tf_op jit(solution)/shard_map/jit(cholesky)/cholesky | solution.py:50
  205.7 0.2 constant_dynamic-update-slice_fusion
  205.9 0.3 convolution_subtract_fusion
  206.2 11.9 %cholesky.105 = f32[128,128]{1,0:T(8,128)S(1)} custom-call(f32[128,128]{1,0:T(8,128)S(1)} %convolution_subtract_fusion), custom_call_target="Cholesky" | custom-call | tf_op jit(solution)/shard_map/jit(cholesky)/cholesky | solution.py:50
  218.1 0.6 compare_reduce_fusion
  220.0 0.1 triangular_solve.73
  220.1 3.8 %while.1 = (s32[]{:T(128)}, f32[256,256]{1,0:T(8,128)S(1)}, s32[2,2]{1,0:T(2,128)S(1)}, f32[2,128,128]{2,1,0:T(8,128)S(1)}, s32[]{:T(128)}) while((s32[]{:T(128)}, f32[256,256]{1,0:T(8,128)S(1)}, s32[2,2]{1,0:T(2,128)S(1)}, f32[2,128,128]{2,1,0:T(8,128)S(1)}, s32[]{:T(128)}) %tuple.28), condition=%wide.while_cond, body=%wide.while_body.sunk | while | flops 2 | bytes 131181 | solution.py:51
  220.1 0.6 fusion.28
  220.7 1.3 bitcast_dynamic-update-slice_fusion.2
  222.0 0.6 fusion.28
  222.6 1.3 bitcast_dynamic-update-slice_fusion.2
  223.9 19.7 %custom-call.17 = f32[2,128,128]{1,2,0:T(8,128)S(1)} custom-call(f32[2,128,128]{2,1,0:T(8,128)S(1)} %get-tuple-element.9), custom_call_target="InvertDiagBlocksLowerTriangular" | custom-call | tf_op jit(solution)/shard_map/triangular_solve | solution.py:51
  243.6 0.4 fusion.4
  244.0 0.6 fusion.13
  244.6 0.4 fusion.3
  245.0 0.3 fusion.10
  245.3 0.3 fusion.15
  245.6 0.3 fusion.7
  246.0 0.8 copy.7
  246.7 0.8 fusion.2
  (12 shorter events, 0.2 us)
Async XLA Ops:
  7.2 75.3 %all-gather.2.cloned.1.call-start = ((), (), s32[]{:S(2)}) async-start(), calls=%async_computation | async-start | bytes 7864320 | tf_op jit(solution)/shard_map/all_gather | solution.py:37
  96.4 24.8 %collective-permute-start = (f32[512,512]{1,0:T(8,128)S(1)}, f32[512,512]{1,0:T(8,128)S(1)}, u32[]{:S(2)}, u32[]{:S(2)}) collective-permute-start(f32[512,512]{1,0:T(8,128)S(1)} %fusion.19), channel_id=1, source_target_pairs={{0,1},{1,0},{2,3},{3,2},{4,5},{5,4},{6,7},{7,6},{8,9},{9,8},{10,11... | collective-permute-start | bytes 3145736 | tf_op jit(solution)/shard_map/ppermute | solution.py:44
  121.5 47.3 %collective-permute-start.1 = (f32[512,512]{1,0:T(8,128)S(1)}, f32[512,512]{1,0:T(8,128)S(1)}, u32[]{:S(2)}, u32[]{:S(2)}) collective-permute-start(f32[512,512]{1,0:T(8,128)S(1)} %add.43), channel_id=1, source_target_pairs={{0,2},{1,3},{2,0},{3,1},{4,6},{5,7},{6,4},{7,5},{8,10},{9,11},{10,... | collective-permute-start | bytes 3145736 | tf_op jit(solution)/shard_map/ppermute | solution.py:44
  170.8 13.0 %collective-permute-start.2 = (f32[256,512]{0,1:T(8,128)S(1)}, f32[256,512]{0,1:T(8,128)S(1)}, u32[]{:S(2)}, u32[]{:S(2)}) collective-permute-start(f32[256,512]{0,1:T(8,128)S(1)} %fusion), channel_id=1, source_target_pairs={{0,4},{4,0},{8,12},{12,8},{1,5},{5,1},{9,13},{13,9},{2,6},{6,2},{1... | collective-permute-start | bytes 1572872 | tf_op jit(solution)/shard_map/ppermute | solution.py:12
Sparse Core Ops, SparseCore 0:
  9.8 72.6 all-gather.1
